TPU v7x, 32 devices: a whole 2x2x4 slice. The times are simulated.
32 devices in a mesh: seq: 16 (over z, y, x), blk: 2 (over core).
Axes of the slice: x: 2, y: 2, z: 4, core: 2. Of those that a mesh axis runs over, the one named last changes fastest.
Arguments:
- query: bfloat16 [2048, 5120], P(('blk', 'seq')), may hold values from -139 to 139
- keys: bfloat16 [2048, 5120], P(('blk', 'seq')), may hold values from -4.5 to 4.5
- values: bfloat16 [2048, 5120], P(('blk', 'seq')), may hold values from -6 to 6
Outputs:
- attended: bfloat16 [2048, 5120], P(('blk', 'seq'))
All inputs are finite; a program needn't handle non-finite values.
Results may differ from a plain program's by a relative error of at most 0.008.
Values may be sent and summed in bfloat16 or wider, within the bound.
A program may use at most 64 MiB of HBM per device.

v0:
```python
import jax
import jax.numpy as jnp
from jax import lax
from jax.sharding import PartitionSpec as P

HEADS = 40


def partner(value, axis, bit):
    mask = 2**bit
    pairs = [(source, source ^ mask) for source in range(lax.axis_size(axis))]
    return lax.ppermute(value, axis, pairs)


def partial_block(q_rows, k_tile, v_tile):
    scores = lax.dot_general(
        q_rows, k_tile, (((1,), (1,)), ((), ())), preferred_element_type=jnp.float32
    ) * q_rows.shape[1] ** (-0.5)
    peak = jnp.max(scores, axis=1)
    expo = jnp.exp(scores - peak[:, None])
    totals = jnp.sum(expo, axis=1)
    summed = jnp.dot(expo.astype(jnp.bfloat16), v_tile, preferred_element_type=jnp.float32)
    return (peak, totals, summed)


def combine_parts(left, right):
    peak = jnp.maximum(left[0], right[0])
    scale_left = jnp.exp(left[0] - peak)
    scale_right = jnp.exp(right[0] - peak)
    totals = scale_left * left[1] + scale_right * right[1]
    summed = scale_left[:, None] * left[2] + scale_right[:, None] * right[2]
    return (peak, totals, summed)


def attend_rows(q_rows, first_k, first_v, second_k, second_v):
    state = partial_block(q_rows, first_k, first_v)
    state = combine_parts(state, partial_block(q_rows, second_k, second_v))
    return (state[2] / state[1][:, None]).astype(jnp.bfloat16)


def attend_item(args):
    q_head, first_k, first_v, second_k, second_v = args
    length, width = q_head.shape
    rows = min(512, length)

    def block(q_rows):
        return attend_rows(q_rows, first_k, first_v, second_k, second_v)

    return lax.map(block, q_head.reshape(length // rows, rows, width)).reshape(length, width)


def items_first(array):
    return jnp.transpose(array.reshape(array.shape[0], array.shape[2], array.shape[3]), (1, 0, 2))


def attend_items(pieces):
    q_group, k_group, v_group = pieces
    q_heads = items_first(q_group)
    k_heads = items_first(k_group)
    v_heads = items_first(v_group)
    stacked = jnp.stack([k_heads, v_heads])
    other = partner(stacked, "blk", 0)
    tiles = (q_heads, k_heads, v_heads, other[0], other[1])
    outcome = lax.map(attend_item, tiles)
    count, length, width = outcome.shape
    outcome = jnp.transpose(outcome, (1, 0, 2)).reshape(length, 1, count, width)
    return lax.all_to_all(outcome, "seq", split_axis=0, concat_axis=1, tiled=True)


def on_device(query, keys, values):
    groups = lax.axis_size("seq")
    width = query.shape[1] // HEADS
    tok_rows = query.shape[0]
    key_source, value_source = (keys, values)
    per_dev = (HEADS + groups - 1) // groups
    slots_all = per_dev * groups

    def split_heads(array):
        count_rows = array.shape[0]
        shaped = array.reshape(count_rows, HEADS, width)
        shaped = jnp.pad(shaped, ((0, 0), (0, slots_all - HEADS), (0, 0)))
        return shaped.reshape(count_rows, groups, per_dev, width)

    result = attend_items(
        (
            lax.all_to_all(split_heads(query), "seq", split_axis=1, concat_axis=0, tiled=True),
            lax.all_to_all(split_heads(key_source), "seq", split_axis=1, concat_axis=0, tiled=True),
            lax.all_to_all(
                split_heads(value_source), "seq", split_axis=1, concat_axis=0, tiled=True
            ),
        )
    )
    result = result.reshape(tok_rows, slots_all, width)[:, :HEADS]
    return result.reshape(tok_rows, HEADS * width)


def solution(mesh):
    placed = (P(("blk", "seq"), None), P(("blk", "seq"), None), P(("blk", "seq"), None))
    return jax.shard_map(
        on_device, mesh=mesh, in_specs=placed, out_specs=P(("blk", "seq"), None), check_vma=False
    )
```

profile of v0, /device:TPU:0, one launch (start us, length us, event | category | flops | bytes accessed | tf_op | source)
XLA Modules:
  0.0 155.3 jit_solution(6471587082868300585)
XLA Ops:
  0.0 1.1 copy-done
  1.3 1.0 pad.11.clone
  2.2 8.3 %all-to-all-start.1 = ((bf16[64,16,3,128]{3,0,2,1:T(8,128)(2,1)}), bf16[64,16,3,128]{3,0,2,1:T(8,128)(2,1)S(1)}, u32[]{:S(2)}, u32[]{:S(2)}) async-start(bf16[64,16,3,128]{3,0,2,1:T(8,128)(2,1)} %bitcast.13), calls=%async_computation.1 | async-start | bytes 1572864 | tf_op jit(solution)/shard_map/all_to_all | solution.py:87
  10.8 1.0 pad.12.clone
  11.8 18.5 %all-to-all-done.1 = bf16[64,16,3,128]{3,0,2,1:T(8,128)(2,1)S(1)} async-done(((bf16[64,16,3,128]{3,0,2,1:T(8,128)(2,1)}), bf16[64,16,3,128]{3,0,2,1:T(8,128)(2,1)S(1)}, u32[]{:S(2)}, u32[]{:S(2)}) %all-to-all-start.1) | async-done | bytes 786464 | tf_op jit(solution)/shard_map/all_to_all | solution.py:87
  30.3 5.0 %all-to-all-start.2 = ((bf16[64,16,3,128]{3,0,2,1:T(8,128)(2,1)}), bf16[64,16,3,128]{3,0,2,1:T(8,128)(2,1)S(1)}, u32[]{:S(2)}, u32[]{:S(2)}) async-start(bf16[64,16,3,128]{3,0,2,1:T(8,128)(2,1)} %bitcast.18), calls=%async_computation.2 | async-start | bytes 1572864 | tf_op jit(solution)/shard_map/all_to_all | solution.py:88
  35.3 18.6 %all-to-all-done.2 = bf16[64,16,3,128]{3,0,2,1:T(8,128)(2,1)S(1)} async-done(((bf16[64,16,3,128]{3,0,2,1:T(8,128)(2,1)}), bf16[64,16,3,128]{3,0,2,1:T(8,128)(2,1)S(1)}, u32[]{:S(2)}, u32[]{:S(2)}) %all-to-all-start.2) | async-done | bytes 786464 | tf_op jit(solution)/shard_map/all_to_all | solution.py:88
  54.8 1.3 copy.18
  56.0 1.3 pad_maximum_fusion
  57.5 1.0 pad.10.clone
  58.5 5.0 %all-to-all-start = ((bf16[64,16,3,128]{3,0,2,1:T(8,128)(2,1)}), bf16[64,16,3,128]{3,0,2,1:T(8,128)(2,1)S(1)}, u32[]{:S(2)}, u32[]{:S(2)}) async-start(bf16[64,16,3,128]{3,0,2,1:T(8,128)(2,1)} %bitcast.121), calls=%async_computation | async-start | bytes 1572864 | tf_op jit(solution)/shard_map/all_to_all | solution.py:86
  63.4 20.1 %all-to-all-done = bf16[64,16,3,128]{3,0,2,1:T(8,128)(2,1)S(1)} async-done(((bf16[64,16,3,128]{3,0,2,1:T(8,128)(2,1)}), bf16[64,16,3,128]{3,0,2,1:T(8,128)(2,1)S(1)}, u32[]{:S(2)}, u32[]{:S(2)}) %all-to-all-start) | async-done | bytes 786464 | tf_op jit(solution)/shard_map/all_to_all | solution.py:86
  84.5 2.6 %slice_bitcast_fusion = (bf16[3,1024,128]{2,1,0:T(8,128)(2,1)}, bf16[3,1024,128]{2,1,0:T(8,128)(2,1)}) fusion(bf16[2,3,1024,128]{3,2,1,0:T(8,128)(2,1)} %collective-permute-done), kind=kLoop, calls=%fused_computation.42 | loop fusion | bytes 3145728 | tf_op jit(solution)/shard_map/squeeze | solution.py:63
  87.1 34.5 %while.21 = (s32[]{:T(128)}, bf16[3,1024,128]{2,1,0:T(8,128)(2,1)}, bf16[3,1024,128]{2,1,0:T(8,128)(2,1)}, bf16[3,1024,128]{2,1,0:T(8,128)(2,1)S(1)}, bf16[3,102...) while((s32[]{:T(128)}, bf16[3,1024,128]{2,1,0:T(8,128)(2,1)}, ...), condition=%wide.region_7.8_spmd, body=%wide.region_0.7_spmd.sunk | while | flops 545588224 | bytes 18780980 | solution.py:64
  87.1 1.0 dynamic-slice_bitcast_fusion.6
  88.1 1.7 %dynamic-slice_bitcast_fusion.7 = (bf16[1024,128]{1,0:T(8,128)(2,1)}, bf16[1024,128]{1,0:T(8,128)(2,1)S(1)}) fusion(bf16[3,1024,128]{2,1,0:T(8,128)(2,1)} %get-tuple-element.302, s32[]{:T(128)} %get-tuple-element.286, bf16[3,1024,128]{2,1,0:T(8,128)(2,1)S(1)} %get-tuple-element.300), kind=kLoop, calls=%fused_computation.35.clone.1 | loop fusion | bytes 1048580 | tf_op jit(solution)/shard_map/while/body/jit(dynamic_index_in_dim)/squeeze | solution.py:64
  89.8 1.0 constant_dynamic-slice_fusion.2
  90.8 7.1 %while.22 = (s32[]{:T(128)}, bf16[2,512,128]{2,1,0:T(8,128)(2,1)S(1)}, bf16[2,512,128]{2,1,0:T(8,128)(2,1)S(1)}, bf16[1024,128]{1,0:T(8,128)(2,1)S(1)}, bf16[102...) while((s32[]{:T(128)}, ...), condition=%wide.region_6.6_spmd, body=%wide.region_1.5_spmd.sunk | while | flops 545588224 | bytes 15634557 | solution.py:49
  91.8 1.0 fusion.50
  95.4 1.0 fusion.50
  98.6 1.0 dynamic-slice_bitcast_fusion.6
  99.6 1.7 %dynamic-slice_bitcast_fusion.7 = (bf16[1024,128]{1,0:T(8,128)(2,1)}, bf16[1024,128]{1,0:T(8,128)(2,1)S(1)}) fusion(bf16[3,1024,128]{2,1,0:T(8,128)(2,1)} %get-tuple-element.302, s32[]{:T(128)} %get-tuple-element.286, bf16[3,1024,128]{2,1,0:T(8,128)(2,1)S(1)} %get-tuple-element.300), kind=kLoop, calls=%fused_computation.35.clone.1 | loop fusion | bytes 1048580 | tf_op jit(solution)/shard_map/while/body/jit(dynamic_index_in_dim)/squeeze | solution.py:64
  101.3 1.0 constant_dynamic-slice_fusion.2
  102.3 7.1 %while.22 = (s32[]{:T(128)}, bf16[2,512,128]{2,1,0:T(8,128)(2,1)S(1)}, bf16[2,512,128]{2,1,0:T(8,128)(2,1)S(1)}, bf16[1024,128]{1,0:T(8,128)(2,1)S(1)}, bf16[102...) while((s32[]{:T(128)}, ...), condition=%wide.region_6.6_spmd, body=%wide.region_1.5_spmd.sunk | while | flops 545588224 | bytes 15634557 | solution.py:49
  103.3 1.0 fusion.50
  110.1 1.0 dynamic-slice_bitcast_fusion.6
  111.1 1.7 %dynamic-slice_bitcast_fusion.7 = (bf16[1024,128]{1,0:T(8,128)(2,1)}, bf16[1024,128]{1,0:T(8,128)(2,1)S(1)}) fusion(bf16[3,1024,128]{2,1,0:T(8,128)(2,1)} %get-tuple-element.302, s32[]{:T(128)} %get-tuple-element.286, bf16[3,1024,128]{2,1,0:T(8,128)(2,1)S(1)} %get-tuple-element.300), kind=kLoop, calls=%fused_computation.35.clone.1 | loop fusion | bytes 1048580 | tf_op jit(solution)/shard_map/while/body/jit(dynamic_index_in_dim)/squeeze | solution.py:64
  112.8 1.0 constant_dynamic-slice_fusion.2
  113.8 7.1 %while.22 = (s32[]{:T(128)}, bf16[2,512,128]{2,1,0:T(8,128)(2,1)S(1)}, bf16[2,512,128]{2,1,0:T(8,128)(2,1)S(1)}, bf16[1024,128]{1,0:T(8,128)(2,1)S(1)}, bf16[102...) while((s32[]{:T(128)}, ...), condition=%wide.region_6.6_spmd, body=%wide.region_1.5_spmd.sunk | while | flops 545588224 | bytes 15634557 | solution.py:49
  114.8 1.0 fusion.50
  121.6 1.8 %copy.35 = bf16[3,1024,128]{2,0,1:T(4,128)(2,1)S(1)} copy(bf16[3,1024,128]{2,1,0:T(8,128)(2,1)} %get-tuple-element.79) | data formatting | bytes 1572864 | tf_op jit(solution)/shard_map/while | solution.py:64
  123.4 30.8 %all_to_all.60 = bf16[1024,1,3,128]{3,2,1,0:T(4,128)(2,1)S(1)} all-to-all(bf16[1024,1,3,128]{3,2,1,0:T(4,128)(2,1)S(1)} %bitcast.116), channel_id=1, replica_groups=mesh['seq'=16,'blk'=2] {'seq'}, dimensions={0} | all-to-all | bytes 1572864 | tf_op jit(solution)/shard_map/all_to_all | solution.py:67
  (68 shorter events, 23.0 us)
Async XLA Ops:
  0.0 1.1 copy-start
  0.0 10.6 %copy-start.3 = (bf16[64,5120]{1,0:T(8,128)(2,1)S(1)}, bf16[64,5120]{1,0:T(8,128)(2,1)}, u32[]{:S(2)}) copy-start(bf16[64,5120]{1,0:T(8,128)(2,1)} %param.9) | copy-start | bytes 1966084
  2.2 28.0 %all-to-all-start.1 = ((bf16[64,16,3,128]{3,0,2,1:T(8,128)(2,1)}), bf16[64,16,3,128]{3,0,2,1:T(8,128)(2,1)S(1)}, u32[]{:S(2)}, u32[]{:S(2)}) async-start(bf16[64,16,3,128]{3,0,2,1:T(8,128)(2,1)} %bitcast.13), calls=%async_computation.1 | async-start | bytes 1572864 | tf_op jit(solution)/shard_map/all_to_all | solution.py:87
  30.3 23.6 %all-to-all-start.2 = ((bf16[64,16,3,128]{3,0,2,1:T(8,128)(2,1)}), bf16[64,16,3,128]{3,0,2,1:T(8,128)(2,1)S(1)}, u32[]{:S(2)}, u32[]{:S(2)}) async-start(bf16[64,16,3,128]{3,0,2,1:T(8,128)(2,1)} %bitcast.18), calls=%async_computation.2 | async-start | bytes 1572864 | tf_op jit(solution)/shard_map/all_to_all | solution.py:88
  53.9 0.9 copy-start.2
  54.8 2.6 %copy-start.4 = (bf16[64,5120]{1,0:T(8,128)(2,1)S(1)}, bf16[64,5120]{1,0:T(8,128)(2,1)}, u32[]{:S(2)}) copy-start(bf16[64,5120]{1,0:T(8,128)(2,1)} %param.7) | copy-start | bytes 1966084
  57.3 27.2 %collective-permute-start = (bf16[2,3,1024,128]{3,2,1,0:T(8,128)(2,1)}, bf16[2,3,1024,128]{3,2,1,0:T(8,128)(2,1)}, u32[]{:S(2)}, u32[]{:S(2)}) collective-permute-start(bf16[2,3,1024,128]{3,2,1,0:T(8,128)(2,1)} %pad_maximum_fusion), channel_id=1, source_target_pairs={{0,1},{1,0},{2,3},{3,2},{4,5},{5,4},{6,7},{7,6},{8,9},{9,8},{10,11... | collective-permute-start | bytes 4718600 | tf_op jit(solution)/shard_map/ppermute | solution.py:12
  58.5 25.1 %all-to-all-start = ((bf16[64,16,3,128]{3,0,2,1:T(8,128)(2,1)}), bf16[64,16,3,128]{3,0,2,1:T(8,128)(2,1)S(1)}, u32[]{:S(2)}, u32[]{:S(2)}) async-start(bf16[64,16,3,128]{3,0,2,1:T(8,128)(2,1)} %bitcast.121), calls=%async_computation | async-start | bytes 1572864 | tf_op jit(solution)/shard_map/all_to_all | solution.py:86
  92.8 1.0 copy-start.1
  96.3 1.0 copy-start.1
  104.3 1.0 copy-start.1
  107.8 1.0 copy-start.1
  115.8 1.0 copy-start.1
  119.3 1.0 copy-start.1
where the time goes:
time: 156 us; the launch traced here: 155 us
  waiting for transfers between devices  57.1 us (37%)
  blocking collectives  30.8 us (20%)
  local copies, waits for them, and re-layouts  28.7 us (18%)
  starting transfers between devices  18.2 us (12%)
  matrix products  12.9 us (8%)
  other arithmetic  7.11 us (5%)
    all_to_all x1, blocking collectives, attend_items(): lax.all_to_all(outcome, 'seq', split_axis=0, concat_axis=1, tiled=True)  30.8 us
    all_to_all x1, waiting for transfers between devices, on_device(): lax.all_to_all(split_heads(query), 'seq', split_axis=1, concat_axis=0, ti...  20.1 us
    all_to_all x1, waiting for transfers between devices, on_device(): lax.all_to_all(split_heads(value_source), 'seq', split_axis=1, concat_axi...  18.6 us
    all_to_all x1, waiting for transfers between devices, on_device(): lax.all_to_all(split_heads(key_source), 'seq', split_axis=1, concat_axis=...  18.5 us
    all_to_all x1, starting transfers between devices, on_device(): lax.all_to_all(split_heads(key_source), 'seq', split_axis=1, concat_axis=...  8.34 us
    squeeze x6, local copies, waits for them, and re-layouts, attend_items(): outcome = lax.map(attend_item, tiles)  8.03 us
    dot_general x12, matrix products, partial_block(): jnp.dot(expo.astype(jnp.bfloat16), v_tile, preferred_element_type=jnp.flo...  6.67 us
    dot_general x12, matrix products, partial_block(): lax.dot_general(q_rows, k_tile, (((1,), (1,)), ((), ())), preferred_eleme...  6.23 us
  transfers between devices with their start and end apart: 4, of which 3 were waited for; matrix products, arithmetic and copies ran while one was open for 2% of the time, Pallas kernels for 0%

commit v1 on v0

v1 whole, which is shorter than its diff:
```python
import functools
import math

import jax
import jax.numpy as jnp
from jax import lax
from jax.experimental import pallas as pl
from jax.experimental.pallas import tpu as pltpu
from jax.sharding import PartitionSpec as P

HEADS = 40
MESH = pl.DeviceIdType.MESH


def send_order(groups):
    return list(range(groups - 1, 0, -1))


def kernel(
    groups, ranks, cores, per_group, width,
    q_in, k_in, v_in, out,
    q_buf, k_buf, v_buf, o_buf,
    send_sem, fwd_sem, o_send, q_sem, k_sem, v_sem, o_sem,
):
    tok = q_in.shape[0]
    me = lax.axis_index("seq")
    blk = lax.axis_index("blk")
    group = me // ranks
    rank = lax.rem(me, ranks)
    order = send_order(groups)
    mine = rank * cores + blk
    scale = width ** (-0.5) * math.log2(math.e)

    def columns(g, h):
        return pl.ds(pl.multiple_of((g * per_group + h) * width, width), width)

    def rows(g):
        return pl.ds(pl.multiple_of(g * tok, tok), tok)

    def spread(h, source, landing, index, recv):
        for offset in order:
            other = group ^ offset
            pltpu.make_async_remote_copy(
                src_ref=source.at[:, columns(other, h)],
                dst_ref=landing.at[index + (rows(group),)],
                send_sem=send_sem.at[h],
                recv_sem=recv,
                device_id={"seq": other * ranks + rank},
                device_id_type=MESH,
            ).start()
        pltpu.make_async_copy(
            source.at[:, columns(group, h)], landing.at[index + (rows(group),)], recv
        ).start()

    def issue(h, _):
        spread(h, k_in, k_buf, (h, mine), k_sem.at[h, mine])
        spread(h, v_in, v_buf, (h, mine), v_sem.at[h, mine])
        spread(h, q_in, q_buf, (h,), q_sem.at[h])
        return 0

    lax.fori_loop(0, per_group, issue, 0)

    def arrived(buf, sem):
        pltpu.make_async_copy(buf, buf, sem).wait()

    def forward(h, buf, sem, part, target):
        pltpu.make_async_remote_copy(
            src_ref=buf.at[h, part],
            dst_ref=buf.at[h, part],
            send_sem=fwd_sem.at[h],
            recv_sem=sem.at[h, part],
            device_id=target,
            device_id_type=MESH,
        ).start()

    def to_cores(h, buf, sem, part):
        for step in range(1, cores):
            forward(h, buf, sem, part, {"blk": lax.rem(blk + step, cores)})

    def to_ranks(h, buf, sem, part):
        for step in range(1, ranks):
            peer = group * ranks + lax.rem(rank + step, ranks)
            forward(h, buf, sem, part, {"seq": peer})

    def update(h, part, state):
        scores = lax.dot_general(
            q_buf[h], k_buf[h, part], (((1,), (1,)), ((), ())),
            preferred_element_type=jnp.float32,
        )
        peak = jnp.max(scores, axis=1, keepdims=True)
        if state is not None:
            peak = jnp.maximum(peak, state[0])
        expo = jnp.exp2((scores - peak) * scale)
        total = jnp.sum(expo, axis=1, keepdims=True)
        summed = jnp.dot(
            expo.astype(jnp.bfloat16), v_buf[h, part], preferred_element_type=jnp.float32
        )
        if state is not None:
            fade = jnp.exp2((state[0] - peak) * scale)
            total += fade * state[1]
            summed += fade * state[2]
        return (peak, total, summed)

    def head(h, _):
        for buf, sem in ((k_buf, k_sem), (v_buf, v_sem)):
            arrived(buf.at[h, mine], sem.at[h, mine])
            to_ranks(h, buf, sem, mine)
            to_cores(h, buf, sem, mine)
        arrived(q_buf.at[h], q_sem.at[h])
        state = update(h, mine, None)

        def take(part, state):
            arrived(k_buf.at[h, part], k_sem.at[h, part])
            arrived(v_buf.at[h, part], v_sem.at[h, part])
            return update(h, part, state)

        for step in range(1, cores):
            state = take(rank * cores + lax.rem(blk + step, cores), state)
        for hop in range(1, ranks):
            base = lax.rem(rank + hop, ranks) * cores
            for buf, sem in ((k_buf, k_sem), (v_buf, v_sem)):
                arrived(buf.at[h, base + blk], sem.at[h, base + blk])
                to_cores(h, buf, sem, base + blk)
            state = update(h, base + blk, state)
            for step in range(1, cores):
                state = take(base + lax.rem(blk + step, cores), state)

        o_buf[h] = (state[2] / state[1]).astype(o_buf.dtype)
        for offset in order:
            other = group ^ offset
            pltpu.make_async_remote_copy(
                src_ref=o_buf.at[h, rows(other)],
                dst_ref=out.at[:, columns(group, h)],
                send_sem=o_send.at[h],
                recv_sem=o_sem.at[h],
                device_id={"seq": other * ranks + rank},
                device_id_type=MESH,
            ).start()
        pltpu.make_async_copy(
            o_buf.at[h, rows(group)], out.at[:, columns(group, h)], o_sem.at[h]
        ).start()
        return 0

    lax.fori_loop(0, per_group, head, 0)

    away = pl.ds(0, (groups - 1) * tok)
    full = groups * tok

    def finish(h, _):
        for _ in range(3):
            arrived(q_buf.at[h, away], send_sem.at[h])
        arrived(q_buf.at[h, away], o_send.at[h])
        count = 2 * (ranks - 1 + ranks * (cores - 1))
        for _ in range(count):
            arrived(q_buf.at[h], fwd_sem.at[h])
        arrived(o_buf.at[h], o_sem.at[h])
        return 0

    del full
    lax.fori_loop(0, per_group, finish, 0)


def on_device(query, keys, values):
    seq = lax.axis_size("seq")
    cores = lax.axis_size("blk")
    tok, columns = query.shape
    width = columns // HEADS
    groups = math.gcd(seq, HEADS)
    ranks = seq // groups
    per_group = HEADS // groups
    parts = ranks * cores
    span = groups * tok
    dtype = query.dtype
    vmem = pl.BlockSpec(memory_space=pltpu.VMEM)
    dma = pltpu.SemaphoreType.DMA
    return pl.pallas_call(
        functools.partial(kernel, groups, ranks, cores, per_group, width),
        out_shape=jax.ShapeDtypeStruct(query.shape, dtype),
        in_specs=[vmem] * 3,
        out_specs=vmem,
        scratch_shapes=[
            pltpu.VMEM((per_group, span, width), dtype),
            pltpu.VMEM((per_group, parts, span, width), dtype),
            pltpu.VMEM((per_group, parts, span, width), dtype),
            pltpu.VMEM((per_group, span, width), dtype),
            dma((per_group,)),
            dma((per_group,)),
            dma((per_group,)),
            dma((per_group,)),
            dma((per_group, parts)),
            dma((per_group, parts)),
            dma((per_group,)),
        ],
        compiler_params=pltpu.CompilerParams(
            has_side_effects=True, vmem_limit_bytes=56 * 1024 * 1024
        ),
    )(query, keys, values)


def solution(mesh):
    spec = P(("blk", "seq"), None)
    return jax.shard_map(
        on_device, mesh=mesh, in_specs=(spec,) * 3, out_specs=spec, check_vma=False
    )
```

time: 156 us -> 80.5 us (0.52)
  Pallas kernels: 0 us -> 78.3 us
  waiting for transfers between devices: 57.1 us -> 0 us
  blocking collectives: 30.8 us -> 0 us
  local copies, waits for them, and re-layouts: 28.7 us -> 1.97 us
  starting transfers between devices: 18.2 us -> 0 us
  matrix products: 12.9 us -> 0 us
  other arithmetic: 7.11 us -> 0 us
    pallas_call x0 -> x1, Pallas kernels: none -> 78.3 us  [on_device(): pl.pallas_call(functools.partial(kernel, groups, ranks, cores, per_group,...]
    all_to_all x3 -> x0, waiting for transfers between devices: 57.1 us -> none  [the longest x1 20.1 us: on_device(): lax.all_to_all(split_heads(query), 'seq', split_axis=1, concat_axis=0, ti...]
    all_to_all x1 -> x0, blocking collectives: 30.8 us -> none  [attend_items(): lax.all_to_all(outcome, 'seq', split_axis=0, concat_axis=1, tiled=True)]
    all_to_all x3 -> x0, starting transfers between devices: 18.2 us -> none  [the longest x1 8.34 us: on_device(): lax.all_to_all(split_heads(key_source), 'seq', split_axis=1, concat_axis=...]
    dot_general x24 -> x0, matrix products: 12.9 us -> none  [the longest x12 6.67 us: partial_block(): jnp.dot(expo.astype(jnp.bfloat16), v_tile, preferred_element_type=jnp.flo...]
    squeeze x7 -> x0, local copies, waits for them, and re-layouts: 10.7 us -> none  [the longest x6 8.03 us: attend_items(): outcome = lax.map(attend_item, tiles)]
    reduce_sum x6 -> x0, other arithmetic: 5.74 us -> none  [partial_block(): totals = jnp.sum(expo, axis=1)]
    while x13 -> x0, local copies, waits for them, and re-layouts: 4.21 us -> none
  transfers between devices with their start and end apart: 4 -> 0, of which waited for: 3 -> 0; matrix products, arithmetic and copies ran while one was open for 2% -> 0% of each run, Pallas kernels for 0% -> 0%
where the time goes in v1:
time: 80.5 us; the launch traced here: 80.3 us
  Pallas kernels  78.3 us (97%)
  local copies, waits for them, and re-layouts  1.97 us (2%)
    pallas_call x1, Pallas kernels, on_device(): pl.pallas_call(functools.partial(kernel, groups, ranks, cores, per_group,...  78.3 us
    unnamed x1, local copies, waits for them, and re-layouts  1.97 us

profile of v1, /device:TPU:0, one launch (start us, length us, event | category | flops | bytes accessed | tf_op | source)
XLA Modules:
  0.0 80.3 jit_solution(7597432255435274637)
XLA Ops:
  0.0 78.3 %shard_map.37 = bf16[64,5120]{1,0:T(8,128)(2,1)} custom-call(bf16[64,5120]{1,0:T(8,128)(2,1)} %q_in.1, bf16[64,5120]{1,0:T(8,128)(2,1)} %k_in.1, bf16[64,5120]{1,0:T(8,128)(2,1)} %v_in.1), custom_call_target="tpu_custom_call" | custom-call | tf_op jit(solution)/shard_map/pallas_call | solution.py:176
  78.3 2.0 %copy.5 = bf16[64,5120]{1,0:T(8,128)(2,1)} copy(bf16[64,5120]{1,0:T(8,128)(2,1)} %shard_map.37) | data formatting | bytes 1310720

commit v2 on v1

--- a/solution.py
+++ b/solution.py
@@ -31,6 +31,16 @@
     mine = rank * cores + blk
     scale = width ** (-0.5) * math.log2(math.e)
 
+    barrier = pltpu.get_barrier_semaphore()
+    peers = [{"seq": (group ^ offset) * ranks + rank} for offset in order]
+    peers += [
+        {"seq": group * ranks + lax.rem(rank + step, ranks)} for step in range(1, ranks)
+    ]
+    peers += [{"blk": lax.rem(blk + step, cores)} for step in range(1, cores)]
+    for peer in peers:
+        pl.semaphore_signal(barrier, inc=1, device_id=peer, device_id_type=MESH)
+    pl.semaphore_wait(barrier, len(peers))
+
     def columns(g, h):
         return pl.ds(pl.multiple_of((g * per_group + h) * width, width), width)
 
@@ -52,13 +62,12 @@
             source.at[:, columns(group, h)], landing.at[index + (rows(group),)], recv
         ).start()
 
-    def issue(h, _):
+    def issue_kv(h):
         spread(h, k_in, k_buf, (h, mine), k_sem.at[h, mine])
         spread(h, v_in, v_buf, (h, mine), v_sem.at[h, mine])
+
+    def issue_q(h):
         spread(h, q_in, q_buf, (h,), q_sem.at[h])
-        return 0
-
-    lax.fori_loop(0, per_group, issue, 0)
 
     def arrived(buf, sem):
         pltpu.make_async_copy(buf, buf, sem).wait()
@@ -101,31 +110,34 @@
             summed += fade * state[2]
         return (peak, total, summed)
 
-    def head(h, _):
+    def near(h):
         for buf, sem in ((k_buf, k_sem), (v_buf, v_sem)):
             arrived(buf.at[h, mine], sem.at[h, mine])
             to_ranks(h, buf, sem, mine)
             to_cores(h, buf, sem, mine)
+
+    def far(h):
+        for hop in range(1, ranks):
+            part = lax.rem(rank + hop, ranks) * cores + blk
+            for buf, sem in ((k_buf, k_sem), (v_buf, v_sem)):
+                arrived(buf.at[h, part], sem.at[h, part])
+                to_cores(h, buf, sem, part)
+
+    def attend(h):
         arrived(q_buf.at[h], q_sem.at[h])
         state = update(h, mine, None)
-
-        def take(part, state):
-            arrived(k_buf.at[h, part], k_sem.at[h, part])
-            arrived(v_buf.at[h, part], v_sem.at[h, part])
-            return update(h, part, state)
-
-        for step in range(1, cores):
-            state = take(rank * cores + lax.rem(blk + step, cores), state)
         for hop in range(1, ranks):
+            state = update(h, lax.rem(rank + hop, ranks) * cores + blk, state)
+        for hop in range(ranks):
             base = lax.rem(rank + hop, ranks) * cores
-            for buf, sem in ((k_buf, k_sem), (v_buf, v_sem)):
-                arrived(buf.at[h, base + blk], sem.at[h, base + blk])
-                to_cores(h, buf, sem, base + blk)
-            state = update(h, base + blk, state)
             for step in range(1, cores):
-                state = take(base + lax.rem(blk + step, cores), state)
-
+                part = base + lax.rem(blk + step, cores)
+                arrived(k_buf.at[h, part], k_sem.at[h, part])
+                arrived(v_buf.at[h, part], v_sem.at[h, part])
+                state = update(h, part, state)
         o_buf[h] = (state[2] / state[1]).astype(o_buf.dtype)
+
+    def give(h):
         for offset in order:
             other = group ^ offset
             pltpu.make_async_remote_copy(
@@ -139,12 +151,38 @@
         pltpu.make_async_copy(
             o_buf.at[h, rows(group)], out.at[:, columns(group, h)], o_sem.at[h]
         ).start()
+
+    last = per_group - 1
+
+    issue_kv(0)
+    issue_q(0)
+    if per_group > 1:
+        issue_kv(1)
+    near(0)
+
+    def head(h, _):
+        @pl.when(h + 2 <= last)
+        def _():
+            issue_kv(h + 2)
+
+        @pl.when(h + 1 <= last)
+        def _():
+            issue_q(h + 1)
+            near(h + 1)
+
+        far(h)
+
+        @pl.when(h >= 1)
+        def _():
+            give(h - 1)
+
+        attend(h)
         return 0
 
     lax.fori_loop(0, per_group, head, 0)
+    give(last)
 
     away = pl.ds(0, (groups - 1) * tok)
-    full = groups * tok
 
     def finish(h, _):
         for _ in range(3):
@@ -156,8 +194,13 @@
         arrived(o_buf.at[h], o_sem.at[h])
         return 0
 
-    del full
     lax.fori_loop(0, per_group, finish, 0)
+
+
+def place(source, out, sem):
+    copy = pltpu.make_async_copy(source, out, sem)
+    copy.start()
+    copy.wait()
 
 
 def on_device(query, keys, values):
@@ -173,10 +216,10 @@
     dtype = query.dtype
     vmem = pl.BlockSpec(memory_space=pltpu.VMEM)
     dma = pltpu.SemaphoreType.DMA
-    return pl.pallas_call(
+    landed = pl.pallas_call(
         functools.partial(kernel, groups, ranks, cores, per_group, width),
         out_shape=jax.ShapeDtypeStruct(query.shape, dtype),
-        in_specs=[vmem] * 3,
+        in_specs=[pl.BlockSpec(memory_space=pl.ANY)] * 3,
         out_specs=vmem,
         scratch_shapes=[
             pltpu.VMEM((per_group, span, width), dtype),
@@ -192,9 +235,19 @@
             dma((per_group,)),
         ],
         compiler_params=pltpu.CompilerParams(
-            has_side_effects=True, vmem_limit_bytes=56 * 1024 * 1024
+            collective_id=0,
+            has_side_effects=True,
+            vmem_limit_bytes=60 * 1024 * 1024,
         ),
     )(query, keys, values)
+    return pl.pallas_call(
+        place,
+        out_shape=jax.ShapeDtypeStruct(query.shape, dtype),
+        in_specs=[vmem],
+        out_specs=pl.BlockSpec(memory_space=pl.ANY),
+        scratch_shapes=[dma],
+        compiler_params=pltpu.CompilerParams(vmem_limit_bytes=4 * 1024 * 1024),
+    )(landed)
 
 
 def solution(mesh):

time: 80.5 us -> 68.2 us (0.85)
  Pallas kernels: 78.3 us -> 67 us
  local copies, waits for them, and re-layouts: 1.97 us -> 1.08 us
    pallas_call x1, Pallas kernels: 78.3 us -> 66.1 us  [on_device(): pl.pallas_call(functools.partial(kernel, groups, ranks, cores, per_group,...]
    unnamed x1 -> x2, local copies, waits for them, and re-layouts: 1.97 us -> 1.08 us
    pallas_call x0 -> x1, Pallas kernels: none -> 0.84 us  [on_device(): pl.pallas_call(place, out_shape=jax.ShapeDtypeStruct(query.shape, dtype),...]
where the time goes in v2:
time: 68.2 us; the launch traced here: 68 us
  Pallas kernels  67 us (98%)
  local copies, waits for them, and re-layouts  1.08 us (2%)
    pallas_call x1, Pallas kernels, on_device(): pl.pallas_call(functools.partial(kernel, groups, ranks, cores, per_group,...  66.1 us

profile of v2, /device:TPU:0, one launch (start us, length us, event | category | flops | bytes accessed | tf_op | source)
XLA Modules:
  0.0 68.0 jit_solution(1709390156428650562)
XLA Ops:
  0.0 66.1 %shard_map.37.source = bf16[64,5120]{1,0:T(8,128)(2,1)} custom-call(bf16[64,5120]{1,0:T(8,128)(2,1)} %q_in.1, bf16[64,5120]{1,0:T(8,128)(2,1)} %k_in.1, bf16[64,5120]{1,0:T(8,128)(2,1)} %v_in.1), custom_call_target="tpu_custom_call" | custom-call | tf_op jit(solution)/shard_map/pallas_call | solution.py:219
  66.1 0.0 copy-start
  66.1 1.1 %copy-done = bf16[64,5120]{1,0:T(8,128)(2,1)S(1)} copy-done((bf16[64,5120]{1,0:T(8,128)(2,1)S(1)}, bf16[64,5120]{1,0:T(8,128)(2,1)}, u32[]{:S(2)}) %copy-start) | copy-done | bytes 655384
  67.2 0.8 %shard_map.38 = bf16[64,5120]{1,0:T(8,128)(2,1)} custom-call(bf16[64,5120]{1,0:T(8,128)(2,1)S(1)} %copy-done), custom_call_target="tpu_custom_call" | custom-call | tf_op jit(solution)/shard_map/pallas_call | solution.py:243
Async XLA Ops:
  66.1 1.1 %copy-start = (bf16[64,5120]{1,0:T(8,128)(2,1)S(1)}, bf16[64,5120]{1,0:T(8,128)(2,1)}, u32[]{:S(2)}) copy-start(bf16[64,5120]{1,0:T(8,128)(2,1)} %shard_map.37.source) | copy-start | bytes 1966084

commit v3 on v2

--- a/solution.py
+++ b/solution.py
@@ -18,9 +18,9 @@
 
 def kernel(
     groups, ranks, cores, per_group, width,
-    q_in, k_in, v_in, out,
-    q_buf, k_buf, v_buf, o_buf,
-    send_sem, fwd_sem, o_send, q_sem, k_sem, v_sem, o_sem,
+    q_hbm, k_hbm, v_hbm, out,
+    q_in, k_in, v_in, q_buf, k_buf, v_buf, o_buf,
+    load_sem, send_sem, fwd_sem, o_send, q_sem, k_sem, v_sem, o_sem,
 ):
     tok = q_in.shape[0]
     me = lax.axis_index("seq")
@@ -30,6 +30,15 @@
     order = send_order(groups)
     mine = rank * cores + blk
     scale = width ** (-0.5) * math.log2(math.e)
+
+    loads = [
+        pltpu.make_async_copy(source, kept, load_sem.at[index])
+        for index, (source, kept) in enumerate(
+            ((k_hbm, k_in), (v_hbm, v_in), (q_hbm, q_in))
+        )
+    ]
+    for load in loads:
+        load.start()
 
     barrier = pltpu.get_barrier_semaphore()
     peers = [{"seq": (group ^ offset) * ranks + rank} for offset in order]
@@ -154,6 +163,8 @@
 
     last = per_group - 1
 
+    for load in loads:
+        load.wait()
     issue_kv(0)
     issue_q(0)
     if per_group > 1:
@@ -216,16 +227,25 @@
     dtype = query.dtype
     vmem = pl.BlockSpec(memory_space=pltpu.VMEM)
     dma = pltpu.SemaphoreType.DMA
+    held = (2 * parts + 2) * per_group * span * width * dtype.itemsize
+    inputs = [
+        pltpu.with_memory_space_constraint(array, pltpu.HBM)
+        for array in (query, keys, values)
+    ]
     landed = pl.pallas_call(
         functools.partial(kernel, groups, ranks, cores, per_group, width),
-        out_shape=jax.ShapeDtypeStruct(query.shape, dtype),
+        out_shape=pltpu.VMEM(query.shape, dtype),
         in_specs=[pl.BlockSpec(memory_space=pl.ANY)] * 3,
         out_specs=vmem,
         scratch_shapes=[
+            pltpu.VMEM(query.shape, dtype),
+            pltpu.VMEM(query.shape, dtype),
+            pltpu.VMEM(query.shape, dtype),
             pltpu.VMEM((per_group, span, width), dtype),
             pltpu.VMEM((per_group, parts, span, width), dtype),
             pltpu.VMEM((per_group, parts, span, width), dtype),
             pltpu.VMEM((per_group, span, width), dtype),
+            dma((3,)),
             dma((per_group,)),
             dma((per_group,)),
             dma((per_group,)),
@@ -237,9 +257,9 @@
         compiler_params=pltpu.CompilerParams(
             collective_id=0,
             has_side_effects=True,
-            vmem_limit_bytes=60 * 1024 * 1024,
+            vmem_limit_bytes=held + 12 * 1024 * 1024,
         ),
-    )(query, keys, values)
+    )(*inputs)
     return pl.pallas_call(
         place,
         out_shape=jax.ShapeDtypeStruct(query.shape, dtype),

time: 68.2 us -> 65.9 us (0.966)
  Pallas kernels: 67 us -> 65.7 us
  local copies, waits for them, and re-layouts: 1.08 us -> 0 us
    pallas_call x1, Pallas kernels: 66.1 us -> 64.9 us  [on_device(): pl.pallas_call(functools.partial(kernel, groups, ranks, cores, per_group,...]
    unnamed x2 -> x0, local copies, waits for them, and re-layouts: 1.08 us -> none
where the time goes in v3:
time: 65.9 us; the launch traced here: 65.8 us
  Pallas kernels  65.7 us (100%)
    pallas_call x1, Pallas kernels, on_device(): pl.pallas_call(functools.partial(kernel, groups, ranks, cores, per_group,...  64.9 us

profile of v3, /device:TPU:0, one launch (start us, length us, event | category | flops | bytes accessed | tf_op | source)
XLA Modules:
  0.0 65.8 jit_solution(1893061142203367153)
XLA Ops:
  0.0 64.9 %shard_map.37.source = bf16[64,5120]{1,0:T(8,128)(2,1)S(1)} custom-call(bf16[64,5120]{1,0:T(8,128)(2,1)} %q_hbm.1, bf16[64,5120]{1,0:T(8,128)(2,1)} %k_hbm.1, bf16[64,5120]{1,0:T(8,128)(2,1)} %v_hbm.1), custom_call_target="tpu_custom_call" | custom-call | tf_op jit(solution)/shard_map/pallas_call | solution.py:235
  64.9 0.8 %shard_map.38 = bf16[64,5120]{1,0:T(8,128)(2,1)} custom-call(bf16[64,5120]{1,0:T(8,128)(2,1)S(1)} %shard_map.37.source), custom_call_target="tpu_custom_call" | custom-call | tf_op jit(solution)/shard_map/pallas_call | solution.py:263

commit v4 on v3

--- a/solution.py
+++ b/solution.py
@@ -13,7 +13,7 @@
 
 
 def send_order(groups):
-    return list(range(groups - 1, 0, -1))
+    return sorted(range(1, groups), key=lambda o: (-(o % 4 >= 2), -o))
 
 
 def kernel(
@@ -163,9 +163,10 @@
 
     last = per_group - 1
 
-    for load in loads:
-        load.wait()
+    loads[0].wait()
+    loads[1].wait()
     issue_kv(0)
+    loads[2].wait()
     issue_q(0)
     if per_group > 1:
         issue_kv(1)
@@ -181,11 +182,11 @@
             issue_q(h + 1)
             near(h + 1)
 
-        far(h)
-
         @pl.when(h >= 1)
         def _():
             give(h - 1)
+
+        far(h)
 
         attend(h)
         return 0

time: 65.9 us -> 65.7 us (level)
  no operation moved by 1% of the time
where the time goes in v4:
time: 65.7 us; the launch traced here: 65.6 us
  Pallas kernels  65.6 us (100%)
    pallas_call x1, Pallas kernels, on_device(): pl.pallas_call(functools.partial(kernel, groups, ranks, cores, per_group,...  64.7 us

profile of v4, /device:TPU:0, one launch (start us, length us, event | category | flops | bytes accessed | tf_op | source)
XLA Modules:
  0.0 65.6 jit_solution(14490239425465738037)
XLA Ops:
  0.0 64.7 %shard_map.37.source = bf16[64,5120]{1,0:T(8,128)(2,1)S(1)} custom-call(bf16[64,5120]{1,0:T(8,128)(2,1)} %q_hbm.1, bf16[64,5120]{1,0:T(8,128)(2,1)} %k_hbm.1, bf16[64,5120]{1,0:T(8,128)(2,1)} %v_hbm.1), custom_call_target="tpu_custom_call" | custom-call | tf_op jit(solution)/shard_map/pallas_call | solution.py:236
  64.8 0.8 %shard_map.38 = bf16[64,5120]{1,0:T(8,128)(2,1)} custom-call(bf16[64,5120]{1,0:T(8,128)(2,1)S(1)} %shard_map.37.source), custom_call_target="tpu_custom_call" | custom-call | tf_op jit(solution)/shard_map/pallas_call | solution.py:264
